TPU v7x, 128 devices: a whole 4x4x4 slice. The times are simulated.
128 devices in a mesh: dp: 64 (over z_hi, x, y, core), mp: 2 (over z_lo).
Axes of the slice: x: 4, y: 4, z: 4 (z_hi: 2, z_lo: 2; z = z_hi * 2 + z_lo), core: 2. Of those that a mesh axis runs over, the one named last changes fastest.
Arguments:
- inputs: bfloat16 [8192, 1792], P('dp', 'mp'), may hold values from -6 to 6
- cotangent: bfloat16 [8192, 1792], P('dp', 'mp'), may hold values from -6 to 6
- gate_weight: bfloat16 [9472, 1792], P(('mp', 'dp')), may hold values from -0.125 to 0.125
- up_weight: bfloat16 [9472, 1792], P(('mp', 'dp')), may hold values from -0.125 to 0.125
- down_weight: bfloat16 [9472, 1792], P(('mp', 'dp')), may hold values from -0.0625 to 0.0625
Outputs:
- input_grad: bfloat16 [8192, 1792], P('dp', 'mp')
- gate_grad: bfloat16 [9472, 1792], P(('mp', 'dp'))
All inputs are finite; a program needn't handle non-finite values.
Results may differ from a plain program's by a relative error of at most 0.009.
Values may be sent and summed in bfloat16 or wider, within the bound.
A program may use at most 320 MiB of HBM per device.

v0:
```python
import jax
import jax.numpy as jnp
from jax import lax
from jax.sharding import Mesh
from jax.sharding import PartitionSpec as P

DP = ("dp_0", "dp_1", "dp_2", "dp_3")
MP_DP = ("mp", "dp_0", "dp_1", "dp_2", "dp_3")
TOK = ("dp_0", "dp_1", "mp")
HID = ("dp_2", "dp_3")


def tdot(left, right):
    return lax.dot_general(
        left, right, (((0,), (0,)), ((), ())), preferred_element_type=jnp.float32
    )


def rdot(left, right):
    return lax.dot_general(
        left, right, (((1,), (1,)), ((), ())), preferred_element_type=jnp.float32
    )


def whole_rows(pieces):
    groups, rows, width = pieces.shape
    halves = pieces.reshape(groups // 2, 2, rows, width)
    return jnp.moveaxis(halves, 1, 2).reshape(groups // 2 * rows, 2 * width)


def per_device(inputs, cotangent, gate_weight, up_weight, down_weight):
    rows, half = inputs.shape
    full_in = whole_rows(lax.all_gather(inputs, TOK, axis=0))
    full_cot = whole_rows(lax.all_gather(cotangent, TOK, axis=0))
    wg = lax.all_gather(gate_weight, HID, axis=0, tiled=True)
    wu = lax.all_gather(up_weight, HID, axis=0, tiled=True)
    wd = lax.all_gather(down_weight, HID, axis=0, tiled=True)
    gate = rdot(full_in, wg)
    up = rdot(full_in, wu)
    dhidden = rdot(full_cot, wd)
    sig = jax.nn.sigmoid(gate)
    act = gate * sig
    dup = (dhidden * act).astype(jnp.bfloat16)
    dgate = (dhidden * up * sig * (1.0 + gate * (1.0 - sig))).astype(jnp.bfloat16)
    total = jnp.dot(dgate, wg, preferred_element_type=jnp.float32)
    total = total + jnp.dot(dup, wu, preferred_element_type=jnp.float32)
    blocks = total.astype(jnp.bfloat16).reshape(-1, rows, 2, half)
    blocks = jnp.moveaxis(blocks, 2, 1).reshape(-1, rows, half)
    input_grad = lax.psum_scatter(blocks, TOK, scatter_dimension=0)
    gate_sum = tdot(dgate, full_in).astype(jnp.bfloat16)
    gate_grad = lax.psum_scatter(gate_sum, HID, scatter_dimension=0, tiled=True)
    return (input_grad, gate_grad)


def solution(mesh):
    torus = Mesh(
        mesh.devices.reshape(2, 4, 4, 2, mesh.shape["mp"]), ("dp_0", "dp_1", "dp_2", "dp_3", "mp")
    )
    return jax.shard_map(
        per_device,
        mesh=torus,
        in_specs=(P(DP, "mp"), P(DP, "mp"), P(MP_DP, None), P(MP_DP, None), P(MP_DP, None)),
        out_specs=(P(DP, "mp"), P(MP_DP, None)),
        check_vma=False,
    )
```

profile of v0, /device:TPU:2, one launch (start us, length us, event | category | flops | bytes accessed | tf_op | source)
XLA Modules:
  0.0 403.8 jit_solution(16914691176496498846)
XLA Ops:
  7.2 0.0 all-gather.19.cloned.1.call-start
  7.2 0.7 all-gather.19.cloned.1.call-update
  7.9 0.0 all-gather.17.cloned.1.call-start
  7.9 0.7 all-gather.17.cloned.1.call-update
  8.6 0.0 all-gather.15.cloned.1.call-start
  8.7 0.7 all-gather.15.cloned.1.call-update
  9.4 0.0 all-gather.13.cloned.1.call-start
  9.4 0.5 all-gather.13.cloned.1.call-update
  10.0 0.0 all-gather.11.cloned.1.call-start
  10.0 0.5 all-gather.11.cloned.1.call-update
  10.5 0.0 reduce-scatter.4.cloned.1.call-start
  10.6 27.0 %all-gather.19.cloned.1.call-done = bf16[8,74,1792]{2,1,0:T(8,128)(2,1)} async-done(((bf16[1,74,1792]{2,1,0:T(8,128)(2,1)}), bf16[8,74,1792]{2,1,0:T(8,128)(2,1)}) %all-gather.19.cloned.1.call-update) | async-done | bytes 2121744 | tf_op jit(solution)/shard_map/all_gather | solution.py:35
  37.6 1.9 reshape.37
  39.5 25.8 %all-gather.17.cloned.1.call-done = bf16[8,74,1792]{2,1,0:T(8,128)(2,1)} async-done(((bf16[1,74,1792]{2,1,0:T(8,128)(2,1)}), bf16[8,74,1792]{2,1,0:T(8,128)(2,1)}) %all-gather.17.cloned.1.call-update) | async-done | bytes 2121744 | tf_op jit(solution)/shard_map/all_gather | solution.py:36
  65.3 2.9 reshape.35
  68.2 24.8 %all-gather.15.cloned.1.call-done = bf16[8,74,1792]{2,1,0:T(8,128)(2,1)} async-done(((bf16[1,74,1792]{2,1,0:T(8,128)(2,1)}), bf16[8,74,1792]{2,1,0:T(8,128)(2,1)}) %all-gather.15.cloned.1.call-update) | async-done | bytes 2121744 | tf_op jit(solution)/shard_map/all_gather | solution.py:37
  93.0 2.9 reshape.33
  95.9 86.8 %all-gather.13.cloned.1.call-done = bf16[2048,896]{1,0:T(8,128)(2,1)} async-done(((bf16[128,896]{1,0:T(8,128)(2,1)}), bf16[2048,896]{1,0:T(8,128)(2,1)}) %all-gather.13.cloned.1.call-update) | async-done | bytes 3670032 | tf_op jit(solution)/shard_map/all_gather | solution.py:33
  182.6 6.5 %copy.12 = bf16[8,2,128,896]{2,0,3,1:T(8,128)(2,1)} copy(bf16[8,2,128,896]{3,2,1,0:T(8,128)(2,1)} %bitcast.44) | data formatting | bytes 7340032 | tf_op jit(solution)/shard_map/reshape | solution.py:27
  189.1 82.3 %all-gather.11.cloned.1.call-done = bf16[2048,896]{1,0:T(8,128)(2,1)} async-done(((bf16[128,896]{1,0:T(8,128)(2,1)}), bf16[2048,896]{1,0:T(8,128)(2,1)}) %all-gather.11.cloned.1.call-update) | async-done | bytes 3670032 | tf_op jit(solution)/shard_map/all_gather | solution.py:34
  271.5 6.5 %copy.11 = bf16[8,2,128,896]{2,0,3,1:T(8,128)(2,1)} copy(bf16[8,2,128,896]{3,2,1,0:T(8,128)(2,1)} %bitcast.48) | data formatting | bytes 7340032 | tf_op jit(solution)/shard_map/reshape | solution.py:27
  277.9 0.0 copy-start
  277.9 5.2 %fusion.7 = f32[1024,592]{0,1:T(8,128)S(1)} fusion(bf16[592,1792]{1,0:T(8,128)(2,1)} %reshape.33, bf16[224,8,8,128]{3,2,1,0:T(8,128)(2,1)} %bitcast.49), kind=kOutput, calls=%fused_computation.7 | convolution fusion | flops 2172649472 | bytes 8216576 | tf_op jit(solution)/shard_map/dot_general | solution.py:20
  283.1 0.0 copy-done
  283.1 0.0 copy-start.1
  283.1 2.4 fusion.5
  285.5 0.0 copy-done.1
  285.5 2.9 multiply_convert_fusion.1
  288.4 3.1 fusion.20
  291.6 4.9 %add_convert_fusion = bf16[1024,1792]{1,0:T(8,128)(2,1)} fusion(f32[1024,1792]{1,0:T(8,128)S(1)} %fusion.20, bf16[592,1792]{1,0:T(8,128)(2,1)S(1)} %copy-done.1, f32[1024,592]{0,1:T(8,128)S(1)} %fusion.7, f32[1024,592]{0,1:T(8,128)S(1)} %fusion.5), kind=kOutput, calls=%fused_computation | convolution fusion | flops 2179956736 | bytes 17981440 | tf_op jit(solution)/shard_map/dot_general | solution.py:46
  296.5 8.1 %reshape.26 = bf16[8,128,2,896]{3,2,1,0:T(2,128)(2,1)} reshape(bf16[1024,1792]{1,0:T(8,128)(2,1)} %add_convert_fusion) | data formatting | bytes 7340032 | tf_op jit(solution)/shard_map/reshape | solution.py:47
  304.6 4.6 %copy.13 = bf16[8,2,128,896]{3,2,1,0:T(8,128)(2,1)} copy(bf16[8,2,128,896]{3,1,2,0:T(2,128)(2,1)} %bitcast.43) | data formatting | bytes 7340032 | tf_op jit(solution)/shard_map/transpose | solution.py:48
  309.2 0.0 reduce-scatter.4.cloned.1.call-update
  309.2 4.4 %fusion.10 = bf16[592,1792]{1,0:T(8,128)(2,1)S(1)} fusion(bf16[1024,592]{0,1:T(8,128)(2,1)S(1)} %multiply_convert_fusion.1, bf16[224,8,8,128]{3,2,1,0:T(8,128)(2,1)} %bitcast.45), kind=kOutput, calls=%fused_computation.10 | convolution fusion | flops 2173710336 | bytes 7004160 | tf_op jit(solution)/shard_map/dot_general | solution.py:14
  313.7 0.0 copy-start.2
  313.7 23.4 %fusion = bf16[80,1792]{1,0:T(8,128)(2,1)S(1)} fusion(bf16[592,1792]{1,0:T(8,128)(2,1)S(1)} %fusion.10), kind=kCustom, calls=%all-reduce-scatter | all-reduce-scatter fusion | flops 1146881 | bytes 2408960
  337.1 1.3 collective-permute-start
  338.4 0.0 copy-done.2
  338.4 0.6 dynamic-slice.4
  339.7 0.0 collective-permute-done
  339.7 0.9 concatenate
  340.6 0.8 constant_dynamic-slice_fusion
  341.4 55.5 %reduce-scatter.4.cloned.1.call-done = bf16[1,128,896]{2,1,0:T(8,128)(2,1)} async-done(((bf16[16,128,896]{2,1,0:T(8,128)(2,1)}), bf16[1,128,896]{2,1,0:T(8,128)(2,1)}) %reduce-scatter.4.cloned.1.call-update) | async-done | bytes 229392 | tf_op jit(solution)/shard_map/reduce_scatter | solution.py:49
  (1 shorter events, 0.0 us)
Async XLA Ops:
  7.2 30.4 %all-gather.19.cloned.1.call-start = ((), (), s32[]{:S(2)}) async-start(), calls=%async_computation.6 | async-start | bytes 2580480 | tf_op jit(solution)/shard_map/all_gather | solution.py:35
  7.9 57.4 %all-gather.17.cloned.1.call-start = ((), (), s32[]{:S(2)}) async-start(), calls=%async_computation.5 | async-start | bytes 2580480 | tf_op jit(solution)/shard_map/all_gather | solution.py:36
  8.6 84.4 %all-gather.15.cloned.1.call-start = ((), (), s32[]{:S(2)}) async-start(), calls=%async_computation.4 | async-start | bytes 2580480 | tf_op jit(solution)/shard_map/all_gather | solution.py:37
  9.4 173.3 %all-gather.13.cloned.1.call-start = ((), (), s32[]{:S(2)}) async-start(), calls=%async_computation.3 | async-start | bytes 3899392 | tf_op jit(solution)/shard_map/all_gather | solution.py:33
  10.0 261.5 %all-gather.11.cloned.1.call-start = ((), (), s32[]{:S(2)}) async-start(), calls=%async_computation.2 | async-start | bytes 3899392 | tf_op jit(solution)/shard_map/all_gather | solution.py:34
  10.5 386.4 %reduce-scatter.4.cloned.1.call-start = ((), (), s32[]{:S(2)}) async-start(), calls=%async_computation.1 | async-start | bytes 3899392 | tf_op jit(solution)/shard_map/reduce_scatter | solution.py:49
  277.9 5.2 %copy-start = (bf16[8,2,128,896]{2,0,3,1:T(8,128)(2,1)S(1)}, bf16[8,2,128,896]{2,0,3,1:T(8,128)(2,1)}, u32[]{:S(2)}) copy-start(bf16[8,2,128,896]{2,0,3,1:T(8,128)(2,1)} %copy.12) | copy-start | bytes 11010052
  283.1 2.4 copy-start.1
  313.7 24.7 %copy-start.2 = (u32[128]{0:T(128)S(1)}, u32[128]{0:T(128)}, u32[]{:S(2)}) copy-start(u32[128]{0:T(128)} %constant.7) | copy-start | bytes 1540
  337.1 2.6 collective-permute-start
Sparse Core Ops, SparseCore 0:
  9.7 27.8 all-gather.18
  39.3 25.9 all-gather.16
  67.0 25.9 all-gather.14
  94.5 88.0 all-gather.12
  184.1 87.2 all-gather.10
  309.4 87.5 reduce-scatter.3
where the time goes:
time: 405 us; the launch traced here: 404 us
  waiting for transfers between devices  305 us (75%)
  local copies, waits for them, and re-layouts  35.8 us (9%)
  blocking collectives  23.4 us (6%)
  matrix products  22.9 us (6%)
  between operations  14.9 us (4%)
    all_gather x1, waiting for transfers between devices, per_device(): full_in = whole_rows(lax.all_gather(inputs, TOK, axis=0))  86.8 us
    all_gather x1, waiting for transfers between devices, per_device(): full_cot = whole_rows(lax.all_gather(cotangent, TOK, axis=0))  82.3 us
    reduce_scatter x1, waiting for transfers between devices, per_device(): input_grad = lax.psum_scatter(blocks, TOK, scatter_dimension=0)  55.5 us
    all_gather x1, waiting for transfers between devices, per_device(): wg = lax.all_gather(gate_weight, HID, axis=0, tiled=True)  27 us
    all_gather x1, waiting for transfers between devices, per_device(): wu = lax.all_gather(up_weight, HID, axis=0, tiled=True)  25.8 us
    all_gather x1, waiting for transfers between devices, per_device(): wd = lax.all_gather(down_weight, HID, axis=0, tiled=True)  24.8 us
    unnamed x1, blocking collectives  23.4 us
    reshape x2, local copies, waits for them, and re-layouts, whole_rows(): halves = pieces.reshape(groups // 2, 2, rows, width)  13 us
  transfers between devices with their start and end apart: 7, of which 6 were waited for; matrix products, arithmetic and copies ran while one was open for 11% of the time, Pallas kernels for 0%

commit v1 on v0

--- a/solution.py
+++ b/solution.py
@@ -32,7 +32,9 @@
     rows, half = inputs.shape
     full_in = whole_rows(lax.all_gather(inputs, TOK, axis=0))
     full_cot = whole_rows(lax.all_gather(cotangent, TOK, axis=0))
-    wg = lax.all_gather(gate_weight, HID, axis=0, tiled=True)
+    wg = jnp.concatenate(
+        lax.all_to_all(jnp.stack([gate_weight] * lax.axis_size(HID)), HID, 0, 0), axis=0
+    )
     wu = lax.all_gather(up_weight, HID, axis=0, tiled=True)
     wd = lax.all_gather(down_weight, HID, axis=0, tiled=True)
     gate = rdot(full_in, wg)

time: 405 us -> 393 us (0.970)
  waiting for transfers between devices: 305 us -> 251 us
  blocking collectives: 23.4 us -> 66.2 us
    all_to_all x0 -> x1, blocking collectives: none -> 42.8 us  [per_device(): lax.all_to_all(jnp.stack([gate_weight] * lax.axis_size(HID)), HID, 0, 0)]
    all_gather x1 -> x0, waiting for transfers between devices: 27 us -> none  [per_device(): wg = lax.all_gather(gate_weight, HID, axis=0, tiled=True)]
    all_gather x1, waiting for transfers between devices: 25.8 us -> 0.01 us  [per_device(): wu = lax.all_gather(up_weight, HID, axis=0, tiled=True)]
    unnamed x13 -> x12, local copies, waits for them, and re-layouts: 10 us -> 7.23 us
  transfers between devices with their start and end apart: 7 -> 6, of which waited for: 6 -> 4; matrix products, arithmetic and copies ran while one was open for 11% -> 11% of each run, Pallas kernels for 0% -> 0%
where the time goes in v1:
time: 393 us; the launch traced here: 392 us
  waiting for transfers between devices  251 us (64%)
  blocking collectives  66.2 us (17%)
  local copies, waits for them, and re-layouts  35.7 us (9%)
  matrix products  22.8 us (6%)
  between operations  14.5 us (4%)
    all_gather x1, waiting for transfers between devices, per_device(): full_in = whole_rows(lax.all_gather(inputs, TOK, axis=0))  86.8 us
    all_gather x1, waiting for transfers between devices, per_device(): full_cot = whole_rows(lax.all_gather(cotangent, TOK, axis=0))  82.3 us
    reduce_scatter x1, waiting for transfers between devices, per_device(): input_grad = lax.psum_scatter(blocks, TOK, scatter_dimension=0)  55.6 us
    all_to_all x1, blocking collectives, per_device(): lax.all_to_all(jnp.stack([gate_weight] * lax.axis_size(HID)), HID, 0, 0)  42.8 us
    all_gather x1, waiting for transfers between devices, per_device(): wd = lax.all_gather(down_weight, HID, axis=0, tiled=True)  23.7 us
    unnamed x1, blocking collectives  23.4 us
    reshape x2, local copies, waits for them, and re-layouts, whole_rows(): halves = pieces.reshape(groups // 2, 2, rows, width)  13 us
    dot_general x3, matrix products, rdot(): lax.dot_general(left, right, (((1,), (1,)), ((), ())), preferred_element_...  10.4 us
  transfers between devices with their start and end apart: 6, of which 4 were waited for; matrix products, arithmetic and copies ran while one was open for 11% of the time, Pallas kernels for 0%

profile of v1, /device:TPU:2, one launch (start us, length us, event | category | flops | bytes accessed | tf_op | source)
XLA Modules:
  0.0 391.8 jit_solution(13469461599624406125)
XLA Ops:
  7.2 0.0 all-gather.15.cloned.1.call-start
  7.2 0.7 all-gather.15.cloned.1.call-update
  7.9 0.0 all-gather.13.cloned.1.call-start
  7.9 0.7 all-gather.13.cloned.1.call-update
  8.6 0.0 all-gather.11.cloned.1.call-start
  8.7 0.7 all-gather.11.cloned.1.call-update
  9.4 0.0 all-gather.9.cloned.1.call-start
  9.4 0.5 all-gather.9.cloned.1.call-update
  10.0 0.0 reduce-scatter.4.cloned.1.call-start
  10.0 1.1 stack.2
  11.1 42.8 %all_to_all.5 = bf16[8,74,1792]{2,1,0:T(8,128)(2,1)S(1)} all-to-all(bf16[8,74,1792]{2,1,0:T(8,128)(2,1)S(1)} %stack.2), channel_id=1, replica_groups=mesh['dp_0'=2,'dp_1'=4,'dp_2'=4,'dp_3'=2,'mp'=2] {'dp_2','dp_3'}, dimensions={0} | all-to-all | bytes 4243456 | tf_op jit(solution)/shard_map/all_to_all | solution.py:36
  53.9 1.6 reshape.31
  55.5 0.0 all-gather.15.cloned.1.call-done
  55.5 1.9 reshape.41
  57.4 23.7 %all-gather.13.cloned.1.call-done = bf16[8,74,1792]{2,1,0:T(8,128)(2,1)} async-done(((bf16[1,74,1792]{2,1,0:T(8,128)(2,1)}), bf16[8,74,1792]{2,1,0:T(8,128)(2,1)}) %all-gather.13.cloned.1.call-update) | async-done | bytes 2121744 | tf_op jit(solution)/shard_map/all_gather | solution.py:39
  81.1 3.0 reshape.39
  84.1 86.8 %all-gather.11.cloned.1.call-done = bf16[2048,896]{1,0:T(8,128)(2,1)} async-done(((bf16[128,896]{1,0:T(8,128)(2,1)}), bf16[2048,896]{1,0:T(8,128)(2,1)}) %all-gather.11.cloned.1.call-update) | async-done | bytes 3670032 | tf_op jit(solution)/shard_map/all_gather | solution.py:33
  170.9 6.5 %copy.12 = bf16[8,2,128,896]{2,0,3,1:T(8,128)(2,1)} copy(bf16[8,2,128,896]{3,2,1,0:T(8,128)(2,1)} %bitcast.43) | data formatting | bytes 7340032 | tf_op jit(solution)/shard_map/reshape | solution.py:27
  177.4 82.3 %all-gather.9.cloned.1.call-done = bf16[2048,896]{1,0:T(8,128)(2,1)} async-done(((bf16[128,896]{1,0:T(8,128)(2,1)}), bf16[2048,896]{1,0:T(8,128)(2,1)}) %all-gather.9.cloned.1.call-update) | async-done | bytes 3670032 | tf_op jit(solution)/shard_map/all_gather | solution.py:34
  259.7 6.5 %copy.11 = bf16[8,2,128,896]{2,0,3,1:T(8,128)(2,1)} copy(bf16[8,2,128,896]{3,2,1,0:T(8,128)(2,1)} %bitcast.47) | data formatting | bytes 7340032 | tf_op jit(solution)/shard_map/reshape | solution.py:27
  266.2 0.0 copy-start
  266.2 0.0 copy-start.1
  266.2 5.2 %fusion.7 = f32[1024,592]{0,1:T(8,128)S(1)} fusion(bf16[592,1792]{1,0:T(8,128)(2,1)} %reshape.39, bf16[224,8,8,128]{3,2,1,0:T(8,128)(2,1)} %bitcast.48), kind=kOutput, calls=%fused_computation.7 | convolution fusion | flops 2172649472 | bytes 8216576 | tf_op jit(solution)/shard_map/dot_general | solution.py:20
  271.4 0.0 copy-done
  271.4 0.0 copy-done.1
  271.4 2.4 fusion.5
  273.8 2.9 multiply_convert_fusion.1
  276.7 3.1 fusion.20
  279.8 4.8 %add_convert_fusion = bf16[1024,1792]{1,0:T(8,128)(2,1)} fusion(f32[1024,1792]{1,0:T(8,128)S(1)} %fusion.20, bf16[592,1792]{1,0:T(8,128)(2,1)S(1)} %reshape.41, f32[1024,592]{0,1:T(8,128)S(1)} %fusion.7, f32[1024,592]{0,1:T(8,128)S(1)} %fusion.5), kind=kOutput, calls=%fused_computation | convolution fusion | flops 2179956736 | bytes 17981440 | tf_op jit(solution)/shard_map/dot_general | solution.py:48
  284.6 8.1 %reshape.32 = bf16[8,128,2,896]{3,2,1,0:T(2,128)(2,1)} reshape(bf16[1024,1792]{1,0:T(8,128)(2,1)} %add_convert_fusion) | data formatting | bytes 7340032 | tf_op jit(solution)/shard_map/reshape | solution.py:49
  292.7 4.7 %copy.13 = bf16[8,2,128,896]{3,2,1,0:T(8,128)(2,1)} copy(bf16[8,2,128,896]{3,1,2,0:T(2,128)(2,1)} %bitcast.42) | data formatting | bytes 7340032 | tf_op jit(solution)/shard_map/transpose | solution.py:50
  297.4 0.0 reduce-scatter.4.cloned.1.call-update
  297.4 4.4 %fusion.10 = bf16[592,1792]{1,0:T(8,128)(2,1)S(1)} fusion(bf16[1024,592]{0,1:T(8,128)(2,1)S(1)} %multiply_convert_fusion.1, bf16[224,8,8,128]{3,2,1,0:T(8,128)(2,1)} %bitcast.44), kind=kOutput, calls=%fused_computation.10 | convolution fusion | flops 2173710336 | bytes 7004160 | tf_op jit(solution)/shard_map/dot_general | solution.py:14
  301.9 0.0 copy-start.2
  301.9 23.4 %fusion = bf16[80,1792]{1,0:T(8,128)(2,1)S(1)} fusion(bf16[592,1792]{1,0:T(8,128)(2,1)S(1)} %fusion.10), kind=kCustom, calls=%all-reduce-scatter | all-reduce-scatter fusion | flops 1146881 | bytes 2408960
  325.3 1.3 collective-permute-start
  326.6 0.0 copy-done.2
  326.6 0.6 dynamic-slice.4
  327.8 0.0 collective-permute-done
  327.9 0.9 concatenate
  328.8 0.8 constant_dynamic-slice_fusion
  329.6 55.6 %reduce-scatter.4.cloned.1.call-done = bf16[1,128,896]{2,1,0:T(8,128)(2,1)} async-done(((bf16[16,128,896]{2,1,0:T(8,128)(2,1)}), bf16[1,128,896]{2,1,0:T(8,128)(2,1)}) %reduce-scatter.4.cloned.1.call-update) | async-done | bytes 229392 | tf_op jit(solution)/shard_map/reduce_scatter | solution.py:51
  (1 shorter events, 0.0 us)
Async XLA Ops:
  7.2 48.4 %all-gather.15.cloned.1.call-start = ((), (), s32[]{:S(2)}) async-start(), calls=%async_computation.6 | async-start | bytes 2580480 | tf_op jit(solution)/shard_map/all_gather | solution.py:38
  7.9 73.2 %all-gather.13.cloned.1.call-start = ((), (), s32[]{:S(2)}) async-start(), calls=%async_computation.5 | async-start | bytes 2580480 | tf_op jit(solution)/shard_map/all_gather | solution.py:39
  8.6 162.2 %all-gather.11.cloned.1.call-start = ((), (), s32[]{:S(2)}) async-start(), calls=%async_computation.4 | async-start | bytes 3899392 | tf_op jit(solution)/shard_map/all_gather | solution.py:33
  9.4 250.3 %all-gather.9.cloned.1.call-start = ((), (), s32[]{:S(2)}) async-start(), calls=%async_computation.3 | async-start | bytes 3899392 | tf_op jit(solution)/shard_map/all_gather | solution.py:34
  10.0 375.3 %reduce-scatter.4.cloned.1.call-start = ((), (), s32[]{:S(2)}) async-start(), calls=%async_computation.2 | async-start | bytes 3899392 | tf_op jit(solution)/shard_map/reduce_scatter | solution.py:51
  266.2 5.2 %copy-start = (bf16[8,2,128,896]{2,0,3,1:T(8,128)(2,1)S(1)}, bf16[8,2,128,896]{2,0,3,1:T(8,128)(2,1)}, u32[]{:S(2)}) copy-start(bf16[8,2,128,896]{2,0,3,1:T(8,128)(2,1)} %copy.12) | copy-start | bytes 11010052
  266.2 5.2 %copy-start.1 = (bf16[592,1792]{1,0:T(8,128)(2,1)S(1)}, bf16[592,1792]{1,0:T(8,128)(2,1)}, u32[]{:S(2)}) copy-start(bf16[592,1792]{1,0:T(8,128)(2,1)} %reshape.31) | copy-start | bytes 6365188
  301.9 24.7 %copy-start.2 = (u32[128]{0:T(128)S(1)}, u32[128]{0:T(128)}, u32[]{:S(2)}) copy-start(u32[128]{0:T(128)} %constant.7) | copy-start | bytes 1540
  325.3 2.6 collective-permute-start
Sparse Core Ops, SparseCore 0:
  9.7 44.4 all-gather.14
  55.9 25.1 all-gather.12
  82.8 88.0 all-gather.10
  172.4 87.2 all-gather.8
  297.5 87.6 reduce-scatter.3
